TPU v7x, 32 devices: a whole 2x2x4 slice. The times are simulated.
32 devices in a mesh: group: 4 (over x, core), member: 8 (over z, y).
Axes of the slice: x: 2, y: 2, z: 4, core: 2. Of those that a mesh axis runs over, the one named last changes fastest.
Arguments:
- amplitudes: bfloat16 [128, 512, 128], P(('group', 'member')), may hold values from -6 to 6
- integrals: bfloat16 [7168, 128, 128], P(('group', 'member')), may hold values from -0.0625 to 0.0625
- task_plan: int32 [7168, 3], P(('group', 'member')), may hold values from 0 to 127, as said below
Outputs:
- residual_tiles: float32 [128, 512, 128], P(('group', 'member'))
Inputs may be any that keep to these rules, and one draw needn't show every extreme that they name: `task_plan`: column 0 is the source tile, column 1 the destination tile, column 2 the executing device as index in the order group, then member. Both tiles of a row lie in the same symmetry block of 32 consecutive tiles, and the executor is a device of the group that holds that block. Every device is the executor of exactly 224 rows. The rows of one device name one executor at most 7 times, and name destination tiles held by one device at most 14 times; both bounds are reached in every draw.
All inputs are finite; a program needn't handle non-finite values.
Results may differ from a plain program's by a relative error of at most 0.0003.
Values may be sent and summed in bfloat16 or wider, within the bound.
No kernel may reach another device: no remote copies, remote signals or barrier semaphores. Data moves between devices by JAX's collectives and lax.ppermute only.
A program may use at most 192 MiB of HBM per device.

v0:
```python
import math

import jax
import jax.numpy as jnp
from jax import lax
from jax.sharding import PartitionSpec as P


def place(tiles, labels, target, capacity, devices_all):
    onehot = (target[:, None] == jnp.arange(devices_all, dtype=jnp.int32)[None, :]).astype(
        jnp.int32
    )
    before = jnp.sum(jnp.cumsum(onehot, axis=0) * onehot, axis=1) - 1
    position = target * capacity + before
    sending = (
        jnp.zeros((devices_all * capacity,) + tiles.shape[1:], tiles.dtype).at[position].set(tiles)
    )
    tagged = jnp.zeros((devices_all * capacity, 3), jnp.int32).at[position].set(labels)
    return (sending, tagged)


def deliver(sending, tagged, capacity, groups, members):
    width = sending.shape[-1]
    devices_all = groups * members
    tiles_in, labels_in = (
        lax.all_to_all(
            sending.reshape(devices_all, capacity, width, width),
            ("group", "member"),
            split_axis=0,
            concat_axis=0,
            tiled=True,
        ),
        lax.all_to_all(
            tagged.reshape(devices_all, capacity, 3),
            ("group", "member"),
            split_axis=0,
            concat_axis=0,
            tiled=True,
        ),
    )
    return (
        tiles_in.reshape(devices_all * capacity, width, width),
        labels_in.reshape(devices_all * capacity, 3),
    )


def accumulate(tiles, source, target, block_amps, count_tiles):
    slots = tiles.shape[0]
    width = tiles.shape[-1]
    rows = block_amps.shape[1]
    block = math.gcd(slots, 32)
    turns = slots // block

    def advance(total, pieces):
        piece_tiles, piece_source, piece_target = pieces
        left_rows = jnp.take(block_amps, piece_source, axis=0)
        product = jnp.einsum(
            "brw,bwv->brv", left_rows, piece_tiles, preferred_element_type=jnp.float32
        )
        return (total.at[piece_target].add(product), None)

    start_total = jnp.zeros((count_tiles, rows, width), jnp.float32)
    total, unused = lax.scan(
        advance,
        start_total,
        (
            tiles.reshape(turns, block, width, width),
            source.reshape(turns, block),
            target.reshape(turns, block),
        ),
    )
    return total


def on_device(amplitudes, integrals, task_plan):
    groups = lax.axis_size("group")
    members = lax.axis_size("member")
    devices_all = groups * members
    tile_dev = amplitudes.shape[0]
    tile_grp = tile_dev * members
    tasks = integrals.shape[0]
    peer_cap = (tasks + devices_all - 1) // devices_all
    block_amps = lax.all_gather(amplitudes, "member", axis=0, tiled=True)
    source = task_plan[:, 0] % tile_grp
    valid = jnp.ones((tasks,), jnp.int32)
    target = task_plan[:, 2]
    local_dest = task_plan[:, 1] % tile_grp
    labels = jnp.stack([source, local_dest, valid], axis=1)
    sending, tagged = place(integrals, labels, target, peer_cap, devices_all)
    tiles_in, labels_in = deliver(sending, tagged, peer_cap, groups, members)
    order = jnp.argsort(1 - labels_in[:, 2], stable=True)[:tasks]
    tiles_in = jnp.take(tiles_in, order, axis=0)
    labels_in = jnp.take(labels_in, order, axis=0)
    partial_tiles = accumulate(tiles_in, labels_in[:, 0], labels_in[:, 1], block_amps, tile_grp)
    return lax.psum_scatter(partial_tiles, "member", scatter_dimension=0, tiled=True)


def solution(mesh):
    in_specs = (
        P(("group", "member"), None, None),
        P(("group", "member"), None, None),
        P(("group", "member"), None),
    )
    out_specs = P(("group", "member"), None, None)
    return jax.shard_map(
        on_device, mesh=mesh, in_specs=in_specs, out_specs=out_specs, check_vma=False
    )
```

profile of v0, /device:TPU:0, one launch (start us, length us, event | category | flops | bytes accessed | tf_op | source)
XLA Modules:
  0.0 669.7 jit_solution(12762651075649319922)
XLA Ops:
  6.5 0.7 slice.27
  7.3 0.6 reduce-window.6
  7.8 0.2 slice_reduce_fusion.2
  8.2 0.8 and_select_fusion.1
  9.0 0.1 copy.25
  9.2 1.1 scatter_custom_fusion.1
  10.4 0.1 reshape.107
  10.5 0.7 copy.27
  11.2 7.3 %all-to-all-start = ((s32[32,7,3]{1,2,0:T(4,128)}), s32[32,7,3]{1,2,0:T(4,128)S(1)}, u32[]{:S(2)}, u32[]{:S(2)}) async-start(s32[32,7,3]{1,2,0:T(4,128)} %copy.27), calls=%async_computation | async-start | bytes 131072 | tf_op jit(solution)/shard_map/all_to_all | solution.py:33
  18.5 4.9 broadcast_in_dim.54
  23.4 33.5 %scatter_fusion.1 = bf16[224,128,128]{2,1,0:T(8,128)(2,1)} fusion(bf16[224,128,128]{2,1,0:T(8,128)(2,1)} %broadcast_in_dim.54, s32[224]{0:T(256)S(1)} %bitcast.55, bf16[224,128,128]{2,1,0:T(8,128)(2,1)} %param.6), kind=kCustom, calls=%fused_computation.5 | custom fusion | bytes 22020992 | tf_op jit(solution)/shard_map/scatter | solution.py:16
  56.9 6.0 all-to-all-start.1
  63.0 0.7 all-gather.2.cloned.1.call-update
  63.7 0.1 reshape.108
  63.8 0.1 copy.29
  64.0 3.2 sort.17
  67.2 0.1 broadcast_in_dim.52
  67.3 0.7 gather_fusion.1
  68.0 0.1 broadcast_select_fusion.1
  68.1 0.2 slice_reduce_fusion
  68.3 0.1 reshape_squeeze.7
  68.4 210.0 %all-to-all-done.1 = bf16[32,7,128,128]{3,2,1,0:T(8,128)(2,1)} async-done(((bf16[32,7,128,128]{3,2,1,0:T(8,128)(2,1)}), bf16[32,7,128,128]{3,2,1,0:T(8,128)(2,1)}, u32[]{:S(2)}, u32[]{:S(2)}) %all-to-all-start.1) | async-done | bytes 7340064 | tf_op jit(solution)/shard_map/all_to_all | solution.py:26
  278.4 11.5 %gather_fusion.2 = bf16[224,128,128]{2,1,0:T(8,128)(2,1)} fusion(bf16[224,128,128]{2,1,0:T(8,128)(2,1)} %bitcast.12, s32[1024]{0:T(1024)S(1)} %pad_clamp_fusion.1), kind=kCustom, calls=%fused_computation.2 | custom fusion | bytes 14680960 | tf_op jit(solution)/shard_map/jit(_take)/gather | solution.py:92
  289.9 6.8 %broadcast_select_fusion = bf16[7,32,128,128]{3,2,1,0:T(8,128)(2,1)} fusion(bf16[7,32,128,128]{3,2,1,0:T(8,128)(2,1)} %bitcast.51, pred[7,32]{1,0:T(8,128)(4,1)S(1)} %broadcast_in_dim.52), kind=kLoop, calls=%fused_computation.24 | loop fusion | flops 3670016 | bytes 14680288 | tf_op jit(solution)/shard_map/jit(_take)/select_n | solution.py:92
  296.7 4.2 broadcast_in_dim.47
  300.9 216.5 %while.10 = (s32[]{:T(128)}, f32[32,512,128]{2,1,0:T(8,128)}, s32[7,32]{1,0:T(8,128)S(1)}, s32[7,32]{1,0:T(8,128)S(1)}, bf16[32,512,128]{2,1,0:T(8,128)(2,1)}, /*index=5*/bf16[7,32,128,128]{3,2,1,0:T(8,128)(2,1)}, s32[]{:T(128)}) while((s32[]{:T(128)}, f32[32,512,128]{2,1,0:T(8,128)}, s32[7,32]{1,0:T(8,128)S(1)}, s32[7,32]{1,0:T(8,128)S(1)}, ...), condition=%wide.region_8.9_spmd, body=%wide.region_6.8_spmd.sunk | while | flops 541066624 | bytes 47191200 | solution.py:63
  300.9 5.3 gather_fusion
  306.2 7.0 %fusion.23 = f32[32,512,128]{2,1,0:T(8,128)} fusion(bf16[32,512,128]{2,1,0:T(8,128)(2,1)} %gather_fusion, pred[32]{0:T(512)(128)(4,1)S(1)} %compare_and_fusion.3, bf16[7,32,128,128]{3,2,1,0:T(8,128)(2,1)} %get-tuple-element.119, s32[]{:T(128)S(6)} %copy.38), kind=kOutput, calls=%fused_computation.6.clone.1 | convolution fusion | flops 538968064 | bytes 13631524 | tf_op jit(solution)/shard_map/while/body/eval_jaxpr/brw,bwv->brv/dot_general | solution.py:57
  313.3 18.7 %scatter_fusion = f32[32,512,128]{2,1,0:T(8,128)} fusion(f32[32,512,128]{2,1,0:T(8,128)} %get-tuple-element.108, s32[32]{0:T(128)S(1)} %get-tuple-element.98, f32[32,512,128]{2,1,0:T(8,128)} %fusion.23), kind=kCustom, calls=%fused_computation.3.clone.1 | custom fusion | flops 2097152 | bytes 25165952 | tf_op jit(solution)/shard_map/while/body/eval_jaxpr/scatter-add | solution.py:60
  332.0 5.3 gather_fusion
  337.3 7.0 %fusion.23 = f32[32,512,128]{2,1,0:T(8,128)} fusion(bf16[32,512,128]{2,1,0:T(8,128)(2,1)} %gather_fusion, pred[32]{0:T(512)(128)(4,1)S(1)} %compare_and_fusion.3, bf16[7,32,128,128]{3,2,1,0:T(8,128)(2,1)} %get-tuple-element.119, s32[]{:T(128)S(6)} %copy.38), kind=kOutput, calls=%fused_computation.6.clone.1 | convolution fusion | flops 538968064 | bytes 13631524 | tf_op jit(solution)/shard_map/while/body/eval_jaxpr/brw,bwv->brv/dot_general | solution.py:57
  344.3 18.5 %scatter_fusion = f32[32,512,128]{2,1,0:T(8,128)} fusion(f32[32,512,128]{2,1,0:T(8,128)} %get-tuple-element.108, s32[32]{0:T(128)S(1)} %get-tuple-element.98, f32[32,512,128]{2,1,0:T(8,128)} %fusion.23), kind=kCustom, calls=%fused_computation.3.clone.1 | custom fusion | flops 2097152 | bytes 25165952 | tf_op jit(solution)/shard_map/while/body/eval_jaxpr/scatter-add | solution.py:60
  362.9 5.3 gather_fusion
  368.2 7.0 %fusion.23 = f32[32,512,128]{2,1,0:T(8,128)} fusion(bf16[32,512,128]{2,1,0:T(8,128)(2,1)} %gather_fusion, pred[32]{0:T(512)(128)(4,1)S(1)} %compare_and_fusion.3, bf16[7,32,128,128]{3,2,1,0:T(8,128)(2,1)} %get-tuple-element.119, s32[]{:T(128)S(6)} %copy.38), kind=kOutput, calls=%fused_computation.6.clone.1 | convolution fusion | flops 538968064 | bytes 13631524 | tf_op jit(solution)/shard_map/while/body/eval_jaxpr/brw,bwv->brv/dot_general | solution.py:57
  375.2 18.3 %scatter_fusion = f32[32,512,128]{2,1,0:T(8,128)} fusion(f32[32,512,128]{2,1,0:T(8,128)} %get-tuple-element.108, s32[32]{0:T(128)S(1)} %get-tuple-element.98, f32[32,512,128]{2,1,0:T(8,128)} %fusion.23), kind=kCustom, calls=%fused_computation.3.clone.1 | custom fusion | flops 2097152 | bytes 25165952 | tf_op jit(solution)/shard_map/while/body/eval_jaxpr/scatter-add | solution.py:60
  393.6 5.3 gather_fusion
  398.9 7.0 %fusion.23 = f32[32,512,128]{2,1,0:T(8,128)} fusion(bf16[32,512,128]{2,1,0:T(8,128)(2,1)} %gather_fusion, pred[32]{0:T(512)(128)(4,1)S(1)} %compare_and_fusion.3, bf16[7,32,128,128]{3,2,1,0:T(8,128)(2,1)} %get-tuple-element.119, s32[]{:T(128)S(6)} %copy.38), kind=kOutput, calls=%fused_computation.6.clone.1 | convolution fusion | flops 538968064 | bytes 13631524 | tf_op jit(solution)/shard_map/while/body/eval_jaxpr/brw,bwv->brv/dot_general | solution.py:57
  405.9 18.7 %scatter_fusion = f32[32,512,128]{2,1,0:T(8,128)} fusion(f32[32,512,128]{2,1,0:T(8,128)} %get-tuple-element.108, s32[32]{0:T(128)S(1)} %get-tuple-element.98, f32[32,512,128]{2,1,0:T(8,128)} %fusion.23), kind=kCustom, calls=%fused_computation.3.clone.1 | custom fusion | flops 2097152 | bytes 25165952 | tf_op jit(solution)/shard_map/while/body/eval_jaxpr/scatter-add | solution.py:60
  424.7 5.3 gather_fusion
  430.0 7.0 %fusion.23 = f32[32,512,128]{2,1,0:T(8,128)} fusion(bf16[32,512,128]{2,1,0:T(8,128)(2,1)} %gather_fusion, pred[32]{0:T(512)(128)(4,1)S(1)} %compare_and_fusion.3, bf16[7,32,128,128]{3,2,1,0:T(8,128)(2,1)} %get-tuple-element.119, s32[]{:T(128)S(6)} %copy.38), kind=kOutput, calls=%fused_computation.6.clone.1 | convolution fusion | flops 538968064 | bytes 13631524 | tf_op jit(solution)/shard_map/while/body/eval_jaxpr/brw,bwv->brv/dot_general | solution.py:57
  437.0 18.6 %scatter_fusion = f32[32,512,128]{2,1,0:T(8,128)} fusion(f32[32,512,128]{2,1,0:T(8,128)} %get-tuple-element.108, s32[32]{0:T(128)S(1)} %get-tuple-element.98, f32[32,512,128]{2,1,0:T(8,128)} %fusion.23), kind=kCustom, calls=%fused_computation.3.clone.1 | custom fusion | flops 2097152 | bytes 25165952 | tf_op jit(solution)/shard_map/while/body/eval_jaxpr/scatter-add | solution.py:60
  455.6 5.3 gather_fusion
  460.9 7.0 %fusion.23 = f32[32,512,128]{2,1,0:T(8,128)} fusion(bf16[32,512,128]{2,1,0:T(8,128)(2,1)} %gather_fusion, pred[32]{0:T(512)(128)(4,1)S(1)} %compare_and_fusion.3, bf16[7,32,128,128]{3,2,1,0:T(8,128)(2,1)} %get-tuple-element.119, s32[]{:T(128)S(6)} %copy.38), kind=kOutput, calls=%fused_computation.6.clone.1 | convolution fusion | flops 538968064 | bytes 13631524 | tf_op jit(solution)/shard_map/while/body/eval_jaxpr/brw,bwv->brv/dot_general | solution.py:57
  467.9 18.6 %scatter_fusion = f32[32,512,128]{2,1,0:T(8,128)} fusion(f32[32,512,128]{2,1,0:T(8,128)} %get-tuple-element.108, s32[32]{0:T(128)S(1)} %get-tuple-element.98, f32[32,512,128]{2,1,0:T(8,128)} %fusion.23), kind=kCustom, calls=%fused_computation.3.clone.1 | custom fusion | flops 2097152 | bytes 25165952 | tf_op jit(solution)/shard_map/while/body/eval_jaxpr/scatter-add | solution.py:60
  486.5 5.3 gather_fusion
  491.8 7.0 %fusion.23 = f32[32,512,128]{2,1,0:T(8,128)} fusion(bf16[32,512,128]{2,1,0:T(8,128)(2,1)} %gather_fusion, pred[32]{0:T(512)(128)(4,1)S(1)} %compare_and_fusion.3, bf16[7,32,128,128]{3,2,1,0:T(8,128)(2,1)} %get-tuple-element.119, s32[]{:T(128)S(6)} %copy.38), kind=kOutput, calls=%fused_computation.6.clone.1 | convolution fusion | flops 538968064 | bytes 13631524 | tf_op jit(solution)/shard_map/while/body/eval_jaxpr/brw,bwv->brv/dot_general | solution.py:57
  498.8 18.6 %scatter_fusion = f32[32,512,128]{2,1,0:T(8,128)} fusion(f32[32,512,128]{2,1,0:T(8,128)} %get-tuple-element.108, s32[32]{0:T(128)S(1)} %get-tuple-element.98, f32[32,512,128]{2,1,0:T(8,128)} %fusion.23), kind=kCustom, calls=%fused_computation.3.clone.1 | custom fusion | flops 2097152 | bytes 25165952 | tf_op jit(solution)/shard_map/while/body/eval_jaxpr/scatter-add | solution.py:60
  517.4 145.4 %reduce-scatter.2.cloned.1.call-done = f32[4,512,128]{2,1,0:T(8,128)} async-done(((f32[32,512,128]{2,1,0:T(8,128)}), f32[4,512,128]{2,1,0:T(8,128)}) %reduce-scatter.2.cloned.1.call-update) | async-done | bytes 1048592 | tf_op jit(solution)/shard_map/reduce_scatter | solution.py:95
  (43 shorter events, 0.7 us)
Async XLA Ops:
  11.2 45.7 %all-to-all-start = ((s32[32,7,3]{1,2,0:T(4,128)}), s32[32,7,3]{1,2,0:T(4,128)S(1)}, u32[]{:S(2)}, u32[]{:S(2)}) async-start(s32[32,7,3]{1,2,0:T(4,128)} %copy.27), calls=%async_computation | async-start | bytes 131072 | tf_op jit(solution)/shard_map/all_to_all | solution.py:33
  56.9 221.5 %all-to-all-start.1 = ((bf16[32,7,128,128]{3,2,1,0:T(8,128)(2,1)}), bf16[32,7,128,128]{3,2,1,0:T(8,128)(2,1)}, u32[]{:S(2)}, u32[]{:S(2)}) async-start(bf16[32,7,128,128]{3,2,1,0:T(8,128)(2,1)} %bitcast.50), calls=%async_computation.1 | async-start | bytes 14680064 | tf_op jit(solution)/shard_map/all_to_all | solution.py:26
  62.9 233.8 %all-gather.2.cloned.1.call-start = ((), (), s32[]{:S(2)}) async-start(), calls=%async_computation.3 | async-start | bytes 4718592 | tf_op jit(solution)/shard_map/all_gather | solution.py:83
  63.6 599.2 %reduce-scatter.2.cloned.1.call-start = ((), (), s32[]{:S(2)}) async-start(), calls=%async_computation.4 | async-start | bytes 9437184 | tf_op jit(solution)/shard_map/reduce_scatter | solution.py:95
Sparse Core Ops, SparseCore 0:
  65.8 180.8 all-gather.1
  517.6 145.2 reduce-scatter.1
where the time goes:
time: 671 us; the launch traced here: 670 us
  waiting for transfers between devices  356 us (53%)
  other arithmetic  142 us (21%)
  local copies, waits for them, and re-layouts  95.6 us (14%)
  matrix products  49.1 us (7%)
  between operations  13.5 us (2%)
  starting transfers between devices  13.4 us (2%)
    all_to_all x1, waiting for transfers between devices, deliver(): lax.all_to_all(sending.reshape(devices_all, capacity, width, width), ('gr...  210 us
    reduce_scatter x1, waiting for transfers between devices, on_device(): lax.psum_scatter(partial_tiles, 'member', scatter_dimension=0, tiled=True)  145 us
    scatter-add x7, other arithmetic, advance(): return (total.at[piece_target].add(product), None)  130 us
    dot_general x7, matrix products, advance(): jnp.einsum('brw,bwv->brv', left_rows, piece_tiles, preferred_element_type...  49.1 us
    gather x7, local copies, waits for them, and re-layouts, advance(): left_rows = jnp.take(block_amps, piece_source, axis=0)  37.2 us
    scatter x1, local copies, waits for them, and re-layouts, place(): jnp.zeros((devices_all * capacity,) + tiles.shape[1:], tiles.dtype)  33.5 us
  transfers between devices with their start and end apart: 4, of which 2 were waited for; matrix products, arithmetic and copies ran while one was open for 9% of the time, Pallas kernels for 0%

commit v1 on v0

v1 whole, which is shorter than its diff:
```python
import functools

import jax
import jax.numpy as jnp
from jax import lax
from jax.experimental import pallas as pl
from jax.experimental.pallas import tpu as pltpu
from jax.sharding import PartitionSpec as P


PARTS = (3, 3, 2)
STEPS = 4.0
LEVELS = 32000.0
SMALLEST = 2.0**-110

SMEM = pl.BlockSpec(memory_space=pltpu.SMEM)
VMEM = pl.BlockSpec(memory_space=pltpu.VMEM)
ANY = pl.BlockSpec(memory_space=pl.ANY)


def params(name):
    return dict(compiler_params=pltpu.CompilerParams(vmem_limit_bytes=60 << 20), name=name)


def cost(flops, size):
    return pl.CostEstimate(flops=flops, bytes_accessed=size, transcendentals=0)


def pad16(count):
    return (count + 15) // 16 * 16


def encode(values, into, at, scales, row):
    peak = jnp.maximum(jnp.max(jnp.abs(values), axis=0, keepdims=True), SMALLEST)
    level = jnp.ceil(jnp.log2(peak) * STEPS)
    scales[pl.ds(row, 1), :] = level
    codes = jnp.round(values * (jnp.exp2(level * (-1.0 / STEPS)) * LEVELS))
    into[pl.ds(at, values.shape[0]), :] = codes.astype(jnp.int32).astype(jnp.int16)


def unit(level):
    return jnp.exp2(level * (1.0 / STEPS)) * (1.0 / LEVELS)


def decode(codes, at, rows, scale):
    return codes[pl.ds(at, rows), :].astype(jnp.int32).astype(jnp.float32) * scale


def sort_body(groups, members, tile_grp, cap, width, plan, tiles, order, labels, first, held, count, sem):
    tasks = tiles.shape[0]
    copy = pltpu.make_async_copy(tiles, held, sem)
    copy.start()
    mine = lax.axis_index("group")
    for k in range(groups):
        count[k] = 0
    if groups * cap > tasks:

        def clear(j, carry):
            for k in range(groups):
                order[k * cap + j] = -1
                labels[k, 0, j] = 0
                labels[k, 1, j] = 0
            return carry

        lax.fori_loop(0, cap, clear, 0)

    def assign(i, carry):
        k = (plan[2, i] // members) ^ mine
        at = count[k]
        count[k] = at + 1
        order[k * cap + at] = i
        labels[k, 0, at] = plan[0, i] % tile_grp
        labels[k, 1, at] = plan[1, i] % tile_grp
        return carry

    lax.fori_loop(0, tasks, assign, 0, unroll=4)
    copy.wait()
    pack(groups, cap, 0, [width], order, held, first)


def pack(groups, cap, low, widths, order, held, outs):
    tasks = held.shape[0]
    unroll = 4 if cap % 4 == 0 else 1

    def step(j, carry):
        for k in range(groups):
            for u in range(unroll):
                at = j * unroll + u
                i = order[k * cap + at]
                if groups * cap > tasks:
                    tile = held[jnp.maximum(i, 0)]
                    tile = jnp.where(i >= 0, tile, jnp.zeros_like(tile))
                else:
                    tile = held[i]
                turned = tile[:, low : low + sum(widths)].T
                start = 0
                for c, width in enumerate(widths):
                    outs[c * groups + k][at] = turned[start : start + width]
                    start += width
        return carry

    lax.fori_loop(0, cap // unroll, step, 0)


def first_body(groups, members, tile_grp, cap, width, plan, tiles, order, labels, *rest):
    sort_body(groups, members, tile_grp, cap, width, plan, tiles, order, labels, rest[:groups], *rest[groups:])


def rest_body(groups, cap, low, widths, order, tiles, *outs):
    pack(groups, cap, low, widths, order, tiles, outs)


def contract_body(groups, members, tile_dev, *refs):
    labels, refs = refs[:groups], refs[groups:]
    pieces, refs = refs[:groups], refs[groups:]
    blocks, refs = refs[:members], refs[members:]
    keep, send, held, total, scales, sems = refs[-6:]
    cap, width, _ = pieces[0].shape
    copies = [
        pltpu.make_async_copy(block, held.at[pl.ds(r * tile_dev, tile_dev)], sems.at[r])
        for r, block in enumerate(blocks)
    ]
    for copy in copies:
        copy.start()
    me = lax.axis_index("member")
    total[...] = jnp.zeros_like(total)
    for copy in copies:
        copy.wait()
    unroll = 2 if cap % 2 == 0 else 1

    def step(j, carry):
        found = []
        for u in range(unroll):
            for k in range(groups):
                at = j * unroll + u
                source = labels[k][0, at] ^ (me * tile_dev)
                product = jnp.dot(pieces[k][at], held[source], preferred_element_type=jnp.float32)
                found.append((labels[k][1, at], product))
        for dest, product in found:
            total[dest] += product
        return carry

    lax.fori_loop(0, cap // unroll, step, 0)
    low = me % 2

    def hand(i, carry):
        outer, t = i // tile_dev, i % tile_dev
        stay = (outer * 2 + low) * tile_dev + t
        go = (outer * 2 + 1 - low) * tile_dev + t
        keep[i] = total[stay]
        encode(total[go], send, i * width, scales, i)
        return carry

    count = members // 2 * tile_dev
    scales[...] = jnp.zeros_like(scales)
    lax.fori_loop(0, count, hand, 0)
    send[pl.ds(count * width, scales.shape[0]), :] = scales[...].astype(jnp.int32).astype(jnp.int16)


def middle_body(lines, tile_dev, keep, codes, *refs):
    own, sends, (scales, fresh) = refs[-lines - 2], refs[-lines - 1 : -2], refs[-2:]
    count, width, _ = keep.shape
    scales[...] = codes[pl.ds(count * width, scales.shape[0]), :].astype(jnp.int32).astype(jnp.float32)
    outer = lax.axis_index("member") // 2

    def value(i):
        return keep[i] + decode(codes, i * width, width, unit(scales[pl.ds(i, 1), :]))

    fresh[...] = jnp.zeros_like(fresh)
    for k in range(lines):
        there = outer ^ k
        for t in range(tile_dev):
            i = there * tile_dev + t
            if k == 0:
                own[t] = value(i)
            else:
                encode(value(i), sends[k - 1], t * width, fresh, t)
        if k:
            sends[k - 1][pl.ds(tile_dev * width, fresh.shape[0]), :] = fresh[...].astype(jnp.int32).astype(jnp.int16)


def last_body(chunks, lines, tile_dev, *refs):
    out, scales, sums = refs[-3:]
    low = 0
    for c in range(chunks):
        own, codes = refs[c * lines], refs[c * lines + 1 : (c + 1) * lines]
        width = own.shape[1]
        for k, code in enumerate(codes):
            scales[k] = code[pl.ds(tile_dev * width, scales.shape[1]), :].astype(jnp.int32).astype(jnp.float32)
        for t in range(tile_dev):
            value = own[t]
            for k, code in enumerate(codes):
                value = value + decode(code, t * width, width, unit(scales[k, t : t + 1, :]))
            sums[t, low : low + width, :] = value
        low += width
    for t in range(tile_dev):
        out[t] = sums[t].T


def on_device(amplitudes, integrals, task_plan):
    groups = lax.axis_size("group")
    members = lax.axis_size("member")
    tile_dev, rows, width = amplitudes.shape
    tasks = integrals.shape[0]
    tile_grp = tile_dev * members
    cap = (tasks + groups * members - 1) // (groups * members) * members
    lines = members // 2
    widths = [width // 8 * part for part in PARTS]
    chunks = len(widths)
    bf16, f32, i16, i32 = jnp.bfloat16, jnp.float32, jnp.int16, jnp.int32
    shape = jax.ShapeDtypeStruct

    def swap(x, axis, k):
        size = lax.axis_size(axis)
        return lax.ppermute(x, axis, [(i, i ^ k) for i in range(size)])

    mine = jnp.swapaxes(amplitudes, 1, 2)
    column = [mine]
    for k in range(1, lines):
        near = k & -k
        column.append(swap(column[k - near], "member", 2 * near))
    across = [swap(mine, "member", 1)]
    for k in range(1, lines):
        across.append(swap(column[k], "member", 1))
    blocks = [block for pair in zip(column, across) for block in pair]

    bare = [shape((cap, w, width), bf16) for w in widths]
    outs = pl.pallas_call(
        functools.partial(first_body, groups, members, tile_grp, cap, widths[0]),
        out_shape=[shape((groups * cap,), i32), shape((groups, 2, cap), i32)] + [bare[0]] * groups,
        in_specs=[SMEM, ANY],
        out_specs=[SMEM, SMEM] + [VMEM] * groups,
        scratch_shapes=[
            pltpu.VMEM(integrals.shape, bf16),
            pltpu.SMEM((groups,), i32),
            pltpu.SemaphoreType.DMA,
        ],
        cost_estimate=cost(tasks * width * width, 2 * integrals.size),
        **params("first"),
    )(task_plan.T, integrals)
    order, labels, sent = outs[0], outs[1], list(outs[2:])
    sent += pl.pallas_call(
        functools.partial(rest_body, groups, cap, widths[0], widths[1:]),
        out_shape=[b for b in bare[1:] for _ in range(groups)],
        in_specs=[SMEM, VMEM],
        out_specs=[VMEM] * (groups * (chunks - 1)),
        cost_estimate=cost(tasks * width * width, 2 * integrals.size),
        **params("rest"),
    )(order, integrals)
    labels = [labels[0]] + [swap(labels[k], "group", k) for k in range(1, groups)]
    pieces = [
        [sent[c * groups]]
        + [swap(sent[c * groups + k], "group", k) for k in range(1, groups)]
        for c in range(chunks)
    ]

    count = lines * tile_dev
    keeps, codes, results, owns = [], [], [], []

    def contract(c):
        piece = widths[c]
        token = owns[c - 2 : c - 1] if c >= 2 else []
        keep, send = pl.pallas_call(
            functools.partial(contract_body, groups, members, tile_dev),
            out_shape=[
                shape((count, piece, rows), f32),
                shape((count * piece + pad16(count), rows), i16),
            ],
            in_specs=[SMEM] * groups + [VMEM] * groups + [ANY] * (members + len(token)),
            out_specs=[VMEM] * 2,
            scratch_shapes=[
                pltpu.VMEM((tile_grp, width, rows), bf16),
                pltpu.VMEM((tile_grp, piece, rows), f32),
                pltpu.VMEM((pad16(count), rows), f32),
                pltpu.SemaphoreType.DMA((members,)),
            ],
            cost_estimate=cost(2 * tasks * width * piece * rows, 8 << 20),
            **params("contract"),
        )(*labels, *pieces[c], *blocks, *token)
        keeps.append(keep)
        codes.append(swap(send, "member", 1))

    def middle(c):
        piece = widths[c]
        token = keeps[c + 1 : c + 2]
        out = pl.pallas_call(
            functools.partial(middle_body, lines, tile_dev),
            out_shape=[shape((tile_dev, piece, rows), f32)]
            + [shape((tile_dev * piece + pad16(tile_dev), rows), i16)] * (lines - 1),
            in_specs=[VMEM] * 2 + [ANY] * len(token),
            out_specs=[VMEM] * lines,
            scratch_shapes=[
                pltpu.VMEM((pad16(count), rows), f32),
                pltpu.VMEM((pad16(tile_dev), rows), f32),
            ],
            cost_estimate=cost(count * piece * rows * 20, 4 << 20),
            **params("middle"),
        )(keeps[c], codes[c], *token)
        owns.append(out[0])
        results.append(out[0])
        results.extend(swap(out[k], "member", 2 * k) for k in range(1, lines))

    contract(0)
    for c in range(1, chunks):
        contract(c)
        middle(c - 1)
    middle(chunks - 1)
    return pl.pallas_call(
        functools.partial(last_body, chunks, lines, tile_dev),
        out_shape=shape((tile_dev, rows, width), f32),
        in_specs=[VMEM] * len(results),
        out_specs=VMEM,
        scratch_shapes=[
            pltpu.VMEM((lines - 1, pad16(tile_dev), rows), f32),
            pltpu.VMEM((tile_dev, width, rows), f32),
        ],
        cost_estimate=cost(tile_dev * width * rows * 20, 4 << 20),
        **params("last"),
    )(*results)


def solution(mesh):
    in_specs = (
        P(("group", "member"), None, None),
        P(("group", "member"), None, None),
        P(("group", "member"), None),
    )
    out_specs = P(("group", "member"), None, None)

    return jax.shard_map(on_device, mesh=mesh, in_specs=in_specs, out_specs=out_specs, check_vma=False)
```

time: 671 us -> 195 us (0.29)
  waiting for transfers between devices: 356 us -> 62.2 us
  other arithmetic: 142 us -> 0 us
  local copies, waits for them, and re-layouts: 95.6 us -> 7.26 us
  Pallas kernels: 0 us -> 75.7 us
  matrix products: 49.1 us -> 0 us
  starting transfers between devices: 13.4 us -> 49 us
  between operations: 13.5 us -> 0.26 us
    all_to_all x2 -> x0, waiting for transfers between devices: 210 us -> none  [the longest x1 210 us: deliver(): lax.all_to_all(sending.reshape(devices_all, capacity, width, width), ('gr...]
    reduce_scatter x1 -> x0, waiting for transfers between devices: 145 us -> none  [on_device(): lax.psum_scatter(partial_tiles, 'member', scatter_dimension=0, tiled=True)]
    scatter-add x7 -> x0, other arithmetic: 130 us -> none  [advance(): return (total.at[piece_target].add(product), None)]
    pallas_call x0 -> x9, Pallas kernels: none -> 75.7 us  [the longest x3 41.7 us: contract(): pl.pallas_call(functools.partial(contract_body, groups, members, tile_dev...]
    ppermute x0 -> x31, waiting for transfers between devices: none -> 62.2 us  [swap(): return lax.ppermute(x, axis, [(i, i ^ k) for i in range(size)])]
    gather x9 -> x0, local copies, waits for them, and re-layouts: 49.4 us -> none  [the longest x7 37.2 us: advance(): left_rows = jnp.take(block_amps, piece_source, axis=0)]
    dot_general x7 -> x0, matrix products: 49.1 us -> none  [advance(): jnp.einsum('brw,bwv->brv', left_rows, piece_tiles, preferred_element_type...]
    ppermute x0 -> x31, starting transfers between devices: none -> 49 us  [swap(): return lax.ppermute(x, axis, [(i, i ^ k) for i in range(size)])]
  transfers between devices with their start and end apart: 4 -> 31, of which waited for: 2 -> 12; matrix products, arithmetic and copies ran while one was open for 9% -> 1% of each run, Pallas kernels for 0% -> 37%
where the time goes in v1:
time: 195 us; the launch traced here: 194 us
  Pallas kernels  75.7 us (39%)
  waiting for transfers between devices  62.2 us (32%)
  starting transfers between devices  49 us (25%)
  local copies, waits for them, and re-layouts  7.26 us (4%)
    ppermute x31, waiting for transfers between devices, swap(): return lax.ppermute(x, axis, [(i, i ^ k) for i in range(size)])  62.2 us
    ppermute x31, starting transfers between devices, swap(): return lax.ppermute(x, axis, [(i, i ^ k) for i in range(size)])  49 us
    pallas_call x3, Pallas kernels, contract(): pl.pallas_call(functools.partial(contract_body, groups, members, tile_dev...  41.7 us
    pallas_call x1, Pallas kernels, on_device(): pl.pallas_call(functools.partial(rest_body, groups, cap, widths[0], width...  13.7 us
    pallas_call x1, Pallas kernels, on_device(): pl.pallas_call(functools.partial(first_body, groups, members, tile_grp, c...  8.77 us
    pallas_call x3, Pallas kernels, middle(): pl.pallas_call(functools.partial(middle_body, lines, tile_dev), out_shape...  8.2 us
    unnamed x61, local copies, waits for them, and re-layouts  5.99 us
  transfers between devices with their start and end apart: 31, of which 12 were waited for; matrix products, arithmetic and copies ran while one was open for 1% of the time, Pallas kernels for 37%

profile of v1, /device:TPU:0, one launch (start us, length us, event | category | flops | bytes accessed | tf_op | source)
XLA Modules:
  0.0 194.4 jit_solution(4992766754920721724)
XLA Ops:
  0.0 1.2 copy.4
  1.3 4.1 %collective-permute-start.9 = (bf16[4,128,512]{2,1,0:T(8,128)(2,1)S(1)}, bf16[4,128,512]{2,1,0:T(8,128)(2,1)S(1)}, u32[]{:S(2)}, u32[]{:S(2)}) collective-permute-start(bf16[4,128,512]{2,1,0:T(8,128)(2,1)S(1)} %bitcast.10), channel_id=1, source_target_pairs={{0,4},{1,5},{2,6},{3,7},{4,0},{5,1},{6,2},{7,3},{8,12},{9,13},{10,... | collective-permute-start | bytes 1572872 | tf_op jit(solution)/shard_map/ppermute | solution.py:215
  5.4 1.6 collective-permute-start.7
  7.0 1.5 collective-permute-start.6
  8.5 8.8 %first.1 = (s32[224]{0:T(256)}, s32[4,2,56]{2,1,0:T(2,128)}, bf16[56,48,128]{2,1,0:T(8,128)(2,1)}, bf16[56,48,128]{2,1,0:T(8,128)(2,1)}, bf16[56,48,128]{2,1,0:T(8,128)(2,1)}, /*index=5*/bf16[56,48,128]{2,1,0:T(8,128)(2,1)}) custom-call(s32[3,224]{1,0:T(4,128)} %bitcast.16, bf16[224,128,128]{2,1,0:T(8,128)(2,1)} %tiles.3), custom_call_target="tpu_custom_call" | custom-call | flops 3670016 | bytes 7340032 | tf_op jit(solution)/shard_map/first/pallas_call | solution.py:228
  17.4 11.3 %collective-permute-done.9.refs_12_ = bf16[4,128,512]{2,1,0:T(8,128)(2,1)S(1)} collective-permute-done((bf16[4,128,512]{2,1,0:T(8,128)(2,1)S(1)}, bf16[4,128,512]{2,1,0:T(8,128)(2,1)S(1)}, u32[]{:S(2)}, u32[]{:S(2)}) %collective-permute-start.9) | collective-permute-done | bytes 524320 | tf_op jit(solution)/shard_map/ppermute | solution.py:215
  28.7 0.6 collective-permute-start.11
  29.3 1.3 slice_bitcast_fusion
  30.5 0.8 collective-permute-start.2
  31.4 2.2 %collective-permute-done.2.refs_3_ = s32[2,56]{1,0:T(2,128)S(1)} collective-permute-done((s32[2,56]{1,0:T(2,128)S(1)}, s32[2,56]{1,0:T(2,128)S(1)}, u32[]{:S(2)}, u32[]{:S(2)}) %collective-permute-start.2) | collective-permute-done | bytes 480 | tf_op jit(solution)/shard_map/ppermute | solution.py:215
  33.6 1.5 collective-permute-start.1
  35.0 2.1 %collective-permute-done.1.refs_2_ = s32[2,56]{1,0:T(2,128)S(1)} collective-permute-done((s32[2,56]{1,0:T(2,128)S(1)}, s32[2,56]{1,0:T(2,128)S(1)}, u32[]{:S(2)}, u32[]{:S(2)}) %collective-permute-start.1) | collective-permute-done | bytes 480 | tf_op jit(solution)/shard_map/ppermute | solution.py:215
  37.1 1.2 collective-permute-done.refs_1_
  38.3 1.5 collective-permute-start.4
  39.8 1.6 collective-permute-start.10
  42.3 1.2 collective-permute-start.12
  43.5 13.7 %rest.1 = (bf16[56,48,128]{2,1,0:T(8,128)(2,1)}, bf16[56,48,128]{2,1,0:T(8,128)(2,1)}, bf16[56,48,128]{2,1,0:T(8,128)(2,1)}, bf16[56,48,128]{2,1,0:T(8,128)(2,1)...) custom-call(s32[224]{0:T(256)} %get-tuple-element.44.order, ...), custom_call_target="tpu_custom_call" | custom-call | flops 3670016 | bytes 7340032 | tf_op jit(solution)/shard_map/rest/pallas_call | solution.py:242
  57.3 12.7 %collective-permute-done.5.refs_7_ = bf16[56,48,128]{2,1,0:T(8,128)(2,1)} collective-permute-done((bf16[56,48,128]{2,1,0:T(8,128)(2,1)}, bf16[56,48,128]{2,1,0:T(8,128)(2,1)}, u32[]{:S(2)}, u32[]{:S(2)}) %collective-permute-start.5) | collective-permute-done | bytes 688160 | tf_op jit(solution)/shard_map/ppermute | solution.py:215
  70.1 1.5 collective-permute-start.15
  71.6 0.7 collective-permute-start.16
  72.2 4.5 %collective-permute-done.12.refs_15_ = bf16[4,128,512]{2,1,0:T(8,128)(2,1)S(1)} collective-permute-done((bf16[4,128,512]{2,1,0:T(8,128)(2,1)S(1)}, bf16[4,128,512]{2,1,0:T(8,128)(2,1)S(1)}, u32[]{:S(2)}, u32[]{:S(2)}) %collective-permute-start.12) | collective-permute-done | bytes 524320 | tf_op jit(solution)/shard_map/ppermute | solution.py:215
  76.8 0.8 copy-done.7
  77.5 14.2 %contract.3 = (f32[16,48,512]{2,1,0:T(8,128)}, s16[784,512]{1,0:T(8,128)(2,1)}) custom-call(s32[2,56]{1,0:T(2,128)} %get-tuple-element.72.refs_0_, s32[2,56]{1,0:T(2,128)} %copy-done.26, s32[2,56]{1,0:T(2,128)} %copy-done.25, s32[2,56]{1,0:T(2,128)} %copy-done.24, bf16[56,48,128]{2,1,0:T(8,128)(2,1)} %get-tuple-element.38.refs_4_, ...), custom_call_target="tpu_custom_call" | custom-call | flops 1409286144 | bytes 8388608 | tf_op jit(solution)/shard_map/contract/pallas_call | solution.py:263
  91.7 1.6 collective-permute-start.13
  93.3 1.5 collective-permute-start.22
  95.2 7.9 %collective-permute-done.16.refs_7_ = bf16[56,48,128]{2,1,0:T(8,128)(2,1)} collective-permute-done((bf16[56,48,128]{2,1,0:T(8,128)(2,1)}, bf16[56,48,128]{2,1,0:T(8,128)(2,1)}, u32[]{:S(2)}, u32[]{:S(2)}) %collective-permute-start.16) | collective-permute-done | bytes 688160 | tf_op jit(solution)/shard_map/ppermute | solution.py:215
  103.1 14.2 %contract.4 = (f32[16,48,512]{2,1,0:T(8,128)}, s16[784,512]{1,0:T(8,128)(2,1)}) custom-call(s32[2,56]{1,0:T(2,128)} %get-tuple-element.72.refs_0_, s32[2,56]{1,0:T(2,128)} %copy-done.26, s32[2,56]{1,0:T(2,128)} %copy-done.25, s32[2,56]{1,0:T(2,128)} %copy-done.24, bf16[56,48,128]{2,1,0:T(8,128)(2,1)} %get-tuple-element.45.refs_4_, ...), custom_call_target="tpu_custom_call" | custom-call | flops 1409286144 | bytes 8388608 | tf_op jit(solution)/shard_map/contract/pallas_call | solution.py:263
  117.4 1.6 collective-permute-start.20
  118.9 0.9 copy-done.9
  119.8 2.9 %middle.3 = (f32[4,48,512]{2,1,0:T(8,128)}, s16[208,512]{1,0:T(8,128)(2,1)}, s16[208,512]{1,0:T(8,128)(2,1)}, s16[208,512]{1,0:T(8,128)(2,1)}) custom-call(f32[16,48,512]{2,1,0:T(8,128)} %get-tuple-element.42.keep, s16[784,512]{1,0:T(8,128)(2,1)} %copy-done.9, f32[16,48,512]{2,1,0:T(8,128)} %get-tuple-element.49.refs_0_.keep), custom_call_target="tpu_custom_call" | custom-call | flops 7864320 | bytes 4194304 | tf_op jit(solution)/shard_map/middle/pallas_call | solution.py:286
  122.8 0.7 copy-done.12
  123.9 13.3 %contract.5 = (f32[16,32,512]{2,1,0:T(8,128)}, s16[528,512]{1,0:T(8,128)(2,1)}) custom-call(s32[2,56]{1,0:T(2,128)} %get-tuple-element.72.refs_0_, s32[2,56]{1,0:T(2,128)} %copy-done.26, s32[2,56]{1,0:T(2,128)} %copy-done.25, s32[2,56]{1,0:T(2,128)} %copy-done.24, bf16[56,32,128]{2,1,0:T(8,128)(2,1)} %get-tuple-element.55.refs_4_, ...), custom_call_target="tpu_custom_call" | custom-call | flops 939524096 | bytes 8388608 | tf_op jit(solution)/shard_map/contract/pallas_call | solution.py:263
  137.2 1.2 collective-permute-start.27
  138.4 1.5 collective-permute-start.17
  139.9 2.0 %collective-permute-start.18 = (s16[208,512]{1,0:T(8,128)(2,1)S(1)}, s16[208,512]{1,0:T(8,128)(2,1)S(1)}, u32[]{:S(2)}, u32[]{:S(2)}) collective-permute-start(s16[208,512]{1,0:T(8,128)(2,1)S(1)} %copy-done.28), channel_id=1, source_target_pairs={{0,4},{1,5},{2,6},{3,7},{4,0},{5,1},{6,2},{7,3},{8,12},{9,13},{10,... | collective-permute-start | bytes 638984 | tf_op jit(solution)/shard_map/ppermute | solution.py:215
  141.9 1.5 collective-permute-start.19
  143.3 0.9 copy-done.8
  144.2 2.9 %middle.4 = (f32[4,48,512]{2,1,0:T(8,128)}, s16[208,512]{1,0:T(8,128)(2,1)}, s16[208,512]{1,0:T(8,128)(2,1)}, s16[208,512]{1,0:T(8,128)(2,1)}) custom-call(f32[16,48,512]{2,1,0:T(8,128)} %get-tuple-element.49.refs_0_.keep, s16[784,512]{1,0:T(8,128)(2,1)} %copy-done.8, f32[16,32,512]{2,1,0:T(8,128)} %get-tuple-element.59.refs_0_.keep), custom_call_target="tpu_custom_call" | custom-call | flops 7864320 | bytes 4194304 | tf_op jit(solution)/shard_map/middle/pallas_call | solution.py:286
  147.6 2.8 %collective-permute-done.17.refs_1_ = s16[208,512]{1,0:T(8,128)(2,1)S(1)} collective-permute-done((s16[208,512]{1,0:T(8,128)(2,1)S(1)}, s16[208,512]{1,0:T(8,128)(2,1)S(1)}, u32[]{:S(2)}, u32[]{:S(2)}) %collective-permute-start.17) | collective-permute-done | bytes 213024 | tf_op jit(solution)/shard_map/ppermute | solution.py:215
  150.4 1.2 collective-permute-done.27.codes
  151.7 2.8 %collective-permute-start.26 = (s16[208,512]{1,0:T(8,128)(2,1)}, s16[208,512]{1,0:T(8,128)(2,1)S(1)}, u32[]{:S(2)}, u32[]{:S(2)}) collective-permute-start(s16[208,512]{1,0:T(8,128)(2,1)} %get-tuple-element.63), channel_id=1, source_target_pairs={{0,6},{1,7},{2,4},{3,5},{4,2},{5,3},{6,0},{7,1},{8,14},{9,15},{10,... | collective-permute-start | bytes 638984 | tf_op jit(solution)/shard_map/ppermute | solution.py:215
  154.5 2.4 %middle.5 = (f32[4,32,512]{2,1,0:T(8,128)}, s16[144,512]{1,0:T(8,128)(2,1)}, s16[144,512]{1,0:T(8,128)(2,1)}, s16[144,512]{1,0:T(8,128)(2,1)}) custom-call(f32[16,32,512]{2,1,0:T(8,128)} %get-tuple-element.59.refs_0_.keep, s16[528,512]{1,0:T(8,128)(2,1)} %copy-done.11), custom_call_target="tpu_custom_call" | custom-call | flops 5242880 | bytes 4194304 | tf_op jit(solution)/shard_map/middle/pallas_call | solution.py:286
  156.9 0.6 collective-permute-done.18.refs_2_
  157.5 1.1 collective-permute-start.28
  158.6 15.6 %collective-permute-start.29 = (s16[144,512]{1,0:T(8,128)(2,1)}, s16[144,512]{1,0:T(8,128)(2,1)S(1)}, u32[]{:S(2)}, u32[]{:S(2)}) collective-permute-start(s16[144,512]{1,0:T(8,128)(2,1)} %get-tuple-element.67), channel_id=1, source_target_pairs={{0,4},{1,5},{2,6},{3,7},{4,0},{5,1},{6,2},{7,3},{8,12},{9,13},{10,... | collective-permute-start | bytes 442376 | tf_op jit(solution)/shard_map/ppermute | solution.py:215
  174.7 7.9 %collective-permute-done.25.refs_6_ = s16[208,512]{1,0:T(8,128)(2,1)S(1)} collective-permute-done((s16[208,512]{1,0:T(8,128)(2,1)}, s16[208,512]{1,0:T(8,128)(2,1)S(1)}, u32[]{:S(2)}, u32[]{:S(2)}) %collective-permute-start.25) | collective-permute-done | bytes 213024 | tf_op jit(solution)/shard_map/ppermute | solution.py:215
  182.6 7.7 %collective-permute-done.29.refs_10_ = s16[144,512]{1,0:T(8,128)(2,1)S(1)} collective-permute-done((s16[144,512]{1,0:T(8,128)(2,1)}, s16[144,512]{1,0:T(8,128)(2,1)S(1)}, u32[]{:S(2)}, u32[]{:S(2)}) %collective-permute-start.29) | collective-permute-done | bytes 147488 | tf_op jit(solution)/shard_map/ppermute | solution.py:215
  191.1 3.3 %last.1 = f32[4,512,128]{2,1,0:T(8,128)} custom-call(f32[4,48,512]{2,1,0:T(8,128)} %get-tuple-element.50.refs_16_.refs_0_, s16[208,512]{1,0:T(8,128)(2,1)} %copy-done.15, s16[208,512]{1,0:T(8,128)(2,1)} %copy-done.16, s16[208,512]{1,0:T(8,128)(2,1)} %copy-done.17, f32[4,48,512]{2,1,0:T(8,128)} %get-tuple-element.60.refs_4_, s16[208,512]{1,0:T(8,128)(2,1)} %copy-done.18, ...), custom_call_target="tpu_custom_call" | custom-call | flops 5242880 | bytes 4194304 | tf_op jit(solution)/shard_map/last/pallas_call | solution.py:308
  (85 shorter events, 3.5 us)
Async XLA Ops:
  1.3 16.0 %copy-start = (bf16[4,512,128]{1,2,0:T(8,128)(2,1)}, bf16[4,512,128]{1,2,0:T(8,128)(2,1)S(1)}, u32[]{:S(2)}) copy-start(bf16[4,512,128]{1,2,0:T(8,128)(2,1)S(1)} %copy.4) | copy-start | bytes 1572868
  1.3 27.4 %collective-permute-start.9 = (bf16[4,128,512]{2,1,0:T(8,128)(2,1)S(1)}, bf16[4,128,512]{2,1,0:T(8,128)(2,1)S(1)}, u32[]{:S(2)}, u32[]{:S(2)}) collective-permute-start(bf16[4,128,512]{2,1,0:T(8,128)(2,1)S(1)} %bitcast.10), channel_id=1, source_target_pairs={{0,4},{1,5},{2,6},{3,7},{4,0},{5,1},{6,2},{7,3},{8,12},{9,13},{10,... | collective-permute-start | bytes 1572872 | tf_op jit(solution)/shard_map/ppermute | solution.py:215
  5.4 34.4 %collective-permute-start.7 = (bf16[4,128,512]{2,1,0:T(8,128)(2,1)S(1)}, bf16[4,128,512]{2,1,0:T(8,128)(2,1)S(1)}, u32[]{:S(2)}, u32[]{:S(2)}) collective-permute-start(bf16[4,128,512]{2,1,0:T(8,128)(2,1)S(1)} %bitcast.11), channel_id=1, source_target_pairs={{0,2},{1,3},{2,0},{3,1},{4,6},{5,7},{6,4},{7,5},{8,10},{9,11},{10,... | collective-permute-start | bytes 1572872 | tf_op jit(solution)/shard_map/ppermute | solution.py:215
  7.0 32.9 %collective-permute-start.6 = (bf16[4,128,512]{2,1,0:T(8,128)(2,1)S(1)}, bf16[4,128,512]{2,1,0:T(8,128)(2,1)S(1)}, u32[]{:S(2)}, u32[]{:S(2)}) collective-permute-start(bf16[4,128,512]{2,1,0:T(8,128)(2,1)S(1)} %bitcast.12), channel_id=1, source_target_pairs={{0,1},{1,0},{2,3},{3,2},{4,5},{5,4},{6,7},{7,6},{8,9},{9,8},{10,11... | collective-permute-start | bytes 1572872 | tf_op jit(solution)/shard_map/ppermute | solution.py:215
  17.3 24.1 %collective-permute-start.3 = (bf16[56,48,128]{2,1,0:T(8,128)(2,1)}, bf16[56,48,128]{2,1,0:T(8,128)(2,1)S(1)}, u32[]{:S(2)}, u32[]{:S(2)}) collective-permute-start(bf16[56,48,128]{2,1,0:T(8,128)(2,1)} %get-tuple-element.39), channel_id=1, source_target_pairs={{0,8},{8,0},{16,24},{24,16},{1,9},{9,1},{17,25},{25,17},{2,10},{10... | collective-permute-start | bytes 2064392 | tf_op jit(solution)/shard_map/ppermute | solution.py:215
  28.7 28.6 %copy-start.1 = (bf16[4,128,512]{2,1,0:T(8,128)(2,1)}, bf16[4,128,512]{2,1,0:T(8,128)(2,1)S(1)}, u32[]{:S(2)}) copy-start(bf16[4,128,512]{2,1,0:T(8,128)(2,1)S(1)} %collective-permute-done.9.refs_12_) | copy-start | bytes 1572868
  28.7 13.3 %collective-permute-start.11 = (bf16[4,128,512]{2,1,0:T(8,128)(2,1)S(1)}, bf16[4,128,512]{2,1,0:T(8,128)(2,1)S(1)}, u32[]{:S(2)}, u32[]{:S(2)}) collective-permute-start(bf16[4,128,512]{2,1,0:T(8,128)(2,1)S(1)} %collective-permute-done.9.refs_12_), channel_id=1, source_target_pairs={{0,2},{1,3},{2,0},{3,1},{4,6},{5,7},{6,4},{7,5},{8,10},{9,11},{10,... | collective-permute-start | bytes 1572872 | tf_op jit(solution)/shard_map/ppermute | solution.py:215
  30.5 3.0 %collective-permute-start.2 = (s32[2,56]{1,0:T(2,128)S(1)}, s32[2,56]{1,0:T(2,128)S(1)}, u32[]{:S(2)}, u32[]{:S(2)}) collective-permute-start(s32[2,56]{1,0:T(2,128)S(1)} %get-tuple-element.69), channel_id=1, source_target_pairs={{0,24},{8,16},{16,8},{24,0},{1,25},{9,17},{17,9},{25,1},{2,26},{10... | collective-permute-start | bytes 1352 | tf_op jit(solution)/shard_map/ppermute | solution.py:215
  33.5 43.2 %copy-start.24 = (s32[2,56]{1,0:T(2,128)}, s32[2,56]{1,0:T(2,128)S(1)}, u32[]{:S(2)}) copy-start(s32[2,56]{1,0:T(2,128)S(1)} %collective-permute-done.2.refs_3_) | copy-start | bytes 1348
  33.6 3.6 %collective-permute-start.1 = (s32[2,56]{1,0:T(2,128)S(1)}, s32[2,56]{1,0:T(2,128)S(1)}, u32[]{:S(2)}, u32[]{:S(2)}) collective-permute-start(s32[2,56]{1,0:T(2,128)S(1)} %get-tuple-element.70), channel_id=1, source_target_pairs={{0,16},{8,24},{16,0},{24,8},{1,17},{9,25},{17,1},{25,9},{2,18},{10... | collective-permute-start | bytes 1352 | tf_op jit(solution)/shard_map/ppermute | solution.py:215
  37.1 39.6 %copy-start.25 = (s32[2,56]{1,0:T(2,128)}, s32[2,56]{1,0:T(2,128)S(1)}, u32[]{:S(2)}) copy-start(s32[2,56]{1,0:T(2,128)S(1)} %collective-permute-done.1.refs_2_) | copy-start | bytes 1348
  37.1 1.2 collective-permute-start
  38.3 38.5 %copy-start.26 = (s32[2,56]{1,0:T(2,128)}, s32[2,56]{1,0:T(2,128)S(1)}, u32[]{:S(2)}) copy-start(s32[2,56]{1,0:T(2,128)S(1)} %collective-permute-done.refs_1_) | copy-start | bytes 1348
  38.3 19.0 %collective-permute-start.4 = (bf16[56,48,128]{2,1,0:T(8,128)(2,1)}, bf16[56,48,128]{2,1,0:T(8,128)(2,1)}, u32[]{:S(2)}, u32[]{:S(2)}) collective-permute-start(bf16[56,48,128]{2,1,0:T(8,128)(2,1)} %get-tuple-element.40), channel_id=1, source_target_pairs={{0,16},{8,24},{16,0},{24,8},{1,17},{9,25},{17,1},{25,9},{2,18},{10... | collective-permute-start | bytes 2064392 | tf_op jit(solution)/shard_map/ppermute | solution.py:215
  39.8 17.4 %copy-start.2 = (bf16[4,128,512]{2,1,0:T(8,128)(2,1)}, bf16[4,128,512]{2,1,0:T(8,128)(2,1)S(1)}, u32[]{:S(2)}) copy-start(bf16[4,128,512]{2,1,0:T(8,128)(2,1)S(1)} %collective-permute-done.7.refs_10_) | copy-start | bytes 1572868
  39.8 30.3 %collective-permute-start.5 = (bf16[56,48,128]{2,1,0:T(8,128)(2,1)}, bf16[56,48,128]{2,1,0:T(8,128)(2,1)}, u32[]{:S(2)}, u32[]{:S(2)}) collective-permute-start(bf16[56,48,128]{2,1,0:T(8,128)(2,1)} %get-tuple-element.41), channel_id=1, source_target_pairs={{0,24},{8,16},{16,8},{24,0},{1,25},{9,17},{17,9},{25,1},{2,26},{10... | collective-permute-start | bytes 2064392 | tf_op jit(solution)/shard_map/ppermute | solution.py:215
  39.8 17.4 %copy-start.3 = (bf16[4,128,512]{2,1,0:T(8,128)(2,1)}, bf16[4,128,512]{2,1,0:T(8,128)(2,1)S(1)}, u32[]{:S(2)}) copy-start(bf16[4,128,512]{2,1,0:T(8,128)(2,1)S(1)} %collective-permute-done.6.refs_9_) | copy-start | bytes 1572868
  39.8 31.7 %collective-permute-start.10 = (bf16[4,128,512]{2,1,0:T(8,128)(2,1)S(1)}, bf16[4,128,512]{2,1,0:T(8,128)(2,1)S(1)}, u32[]{:S(2)}, u32[]{:S(2)}) collective-permute-start(bf16[4,128,512]{2,1,0:T(8,128)(2,1)S(1)} %collective-permute-done.9.refs_12_), channel_id=1, source_target_pairs={{0,1},{1,0},{2,3},{3,2},{4,5},{5,4},{6,7},{7,6},{8,9},{9,8},{10,11... | collective-permute-start | bytes 1572872 | tf_op jit(solution)/shard_map/ppermute | solution.py:215
  41.4 30.8 %collective-permute-start.8 = (bf16[4,128,512]{2,1,0:T(8,128)(2,1)S(1)}, bf16[4,128,512]{2,1,0:T(8,128)(2,1)S(1)}, u32[]{:S(2)}, u32[]{:S(2)}) collective-permute-start(bf16[4,128,512]{2,1,0:T(8,128)(2,1)S(1)} %collective-permute-done.7.refs_10_), channel_id=1, source_target_pairs={{0,1},{1,0},{2,3},{3,2},{4,5},{5,4},{6,7},{7,6},{8,9},{9,8},{10,11... | collective-permute-start | bytes 1572872 | tf_op jit(solution)/shard_map/ppermute | solution.py:215
  42.3 15.0 %copy-start.4 = (bf16[4,128,512]{2,1,0:T(8,128)(2,1)}, bf16[4,128,512]{2,1,0:T(8,128)(2,1)S(1)}, u32[]{:S(2)}) copy-start(bf16[4,128,512]{2,1,0:T(8,128)(2,1)S(1)} %collective-permute-done.11.refs_14_) | copy-start | bytes 1572868
  42.3 34.5 %collective-permute-start.12 = (bf16[4,128,512]{2,1,0:T(8,128)(2,1)S(1)}, bf16[4,128,512]{2,1,0:T(8,128)(2,1)S(1)}, u32[]{:S(2)}, u32[]{:S(2)}) collective-permute-start(bf16[4,128,512]{2,1,0:T(8,128)(2,1)S(1)} %collective-permute-done.11.refs_14_), channel_id=1, source_target_pairs={{0,1},{1,0},{2,3},{3,2},{4,5},{5,4},{6,7},{7,6},{8,9},{9,8},{10,11... | collective-permute-start | bytes 1572872 | tf_op jit(solution)/shard_map/ppermute | solution.py:215
  57.3 36.1 %collective-permute-start.14 = (bf16[56,48,128]{2,1,0:T(8,128)(2,1)}, bf16[56,48,128]{2,1,0:T(8,128)(2,1)}, u32[]{:S(2)}, u32[]{:S(2)}) collective-permute-start(bf16[56,48,128]{2,1,0:T(8,128)(2,1)} %get-tuple-element.46), channel_id=1, source_target_pairs={{0,8},{8,0},{16,24},{24,16},{1,9},{9,1},{17,25},{25,17},{2,10},{10... | collective-permute-start | bytes 2064392 | tf_op jit(solution)/shard_map/ppermute | solution.py:215
  70.1 24.7 %collective-permute-start.15 = (bf16[56,48,128]{2,1,0:T(8,128)(2,1)}, bf16[56,48,128]{2,1,0:T(8,128)(2,1)}, u32[]{:S(2)}, u32[]{:S(2)}) collective-permute-start(bf16[56,48,128]{2,1,0:T(8,128)(2,1)} %get-tuple-element.47), channel_id=1, source_target_pairs={{0,16},{8,24},{16,0},{24,8},{1,17},{9,25},{17,1},{25,9},{2,18},{10... | collective-permute-start | bytes 2064392 | tf_op jit(solution)/shard_map/ppermute | solution.py:215
  71.6 31.6 %collective-permute-start.16 = (bf16[56,48,128]{2,1,0:T(8,128)(2,1)}, bf16[56,48,128]{2,1,0:T(8,128)(2,1)}, u32[]{:S(2)}, u32[]{:S(2)}) collective-permute-start(bf16[56,48,128]{2,1,0:T(8,128)(2,1)} %get-tuple-element.48), channel_id=1, source_target_pairs={{0,24},{8,16},{16,8},{24,0},{1,25},{9,17},{17,9},{25,1},{2,26},{10... | collective-permute-start | bytes 2064392 | tf_op jit(solution)/shard_map/ppermute | solution.py:215
  91.7 27.2 %collective-permute-start.13 = (s16[784,512]{1,0:T(8,128)(2,1)}, s16[784,512]{1,0:T(8,128)(2,1)S(1)}, u32[]{:S(2)}, u32[]{:S(2)}) collective-permute-start(s16[784,512]{1,0:T(8,128)(2,1)} %get-tuple-element.43), channel_id=1, source_target_pairs={{0,1},{1,0},{2,3},{3,2},{4,5},{5,4},{6,7},{7,6},{8,9},{9,8},{10,11... | collective-permute-start | bytes 2408456 | tf_op jit(solution)/shard_map/ppermute | solution.py:215
  93.3 29.4 %collective-permute-start.21 = (bf16[56,32,128]{2,1,0:T(8,128)(2,1)}, bf16[56,32,128]{2,1,0:T(8,128)(2,1)S(1)}, u32[]{:S(2)}, u32[]{:S(2)}) collective-permute-start(bf16[56,32,128]{2,1,0:T(8,128)(2,1)} %get-tuple-element.56), channel_id=1, source_target_pairs={{0,8},{8,0},{16,24},{24,16},{1,9},{9,1},{17,25},{25,17},{2,10},{10... | collective-permute-start | bytes 1376264 | tf_op jit(solution)/shard_map/ppermute | solution.py:215
  93.3 29.4 %collective-permute-start.22 = (bf16[56,32,128]{2,1,0:T(8,128)(2,1)}, bf16[56,32,128]{2,1,0:T(8,128)(2,1)S(1)}, u32[]{:S(2)}, u32[]{:S(2)}) collective-permute-start(bf16[56,32,128]{2,1,0:T(8,128)(2,1)} %get-tuple-element.57), channel_id=1, source_target_pairs={{0,16},{8,24},{16,0},{24,8},{1,17},{9,25},{17,1},{25,9},{2,18},{10... | collective-permute-start | bytes 1376264 | tf_op jit(solution)/shard_map/ppermute | solution.py:215
  94.8 27.9 %collective-permute-start.23 = (bf16[56,32,128]{2,1,0:T(8,128)(2,1)}, bf16[56,32,128]{2,1,0:T(8,128)(2,1)S(1)}, u32[]{:S(2)}, u32[]{:S(2)}) collective-permute-start(bf16[56,32,128]{2,1,0:T(8,128)(2,1)} %get-tuple-element.58), channel_id=1, source_target_pairs={{0,24},{8,16},{16,8},{24,0},{1,25},{9,17},{17,9},{25,1},{2,26},{10... | collective-permute-start | bytes 1376264 | tf_op jit(solution)/shard_map/ppermute | solution.py:215
  117.4 26.0 %collective-permute-start.20 = (s16[784,512]{1,0:T(8,128)(2,1)}, s16[784,512]{1,0:T(8,128)(2,1)S(1)}, u32[]{:S(2)}, u32[]{:S(2)}) collective-permute-start(s16[784,512]{1,0:T(8,128)(2,1)} %get-tuple-element.54), channel_id=1, source_target_pairs={{0,1},{1,0},{2,3},{3,2},{4,5},{5,4},{6,7},{7,6},{8,9},{9,8},{10,11... | collective-permute-start | bytes 2408456 | tf_op jit(solution)/shard_map/ppermute | solution.py:215
  123.9 14.5 %copy-start.29 = (s16[208,512]{1,0:T(8,128)(2,1)S(1)}, s16[208,512]{1,0:T(8,128)(2,1)}, u32[]{:S(2)}) copy-start(s16[208,512]{1,0:T(8,128)(2,1)} %get-tuple-element.51) | copy-start | bytes 638980
  123.9 16.0 %copy-start.28 = (s16[208,512]{1,0:T(8,128)(2,1)S(1)}, s16[208,512]{1,0:T(8,128)(2,1)}, u32[]{:S(2)}) copy-start(s16[208,512]{1,0:T(8,128)(2,1)} %get-tuple-element.52) | copy-start | bytes 638980
  123.9 18.0 %copy-start.27 = (s16[208,512]{1,0:T(8,128)(2,1)S(1)}, s16[208,512]{1,0:T(8,128)(2,1)}, u32[]{:S(2)}) copy-start(s16[208,512]{1,0:T(8,128)(2,1)} %get-tuple-element.53) | copy-start | bytes 638980
  137.2 14.5 %collective-permute-start.27 = (s16[528,512]{1,0:T(8,128)(2,1)}, s16[528,512]{1,0:T(8,128)(2,1)S(1)}, u32[]{:S(2)}, u32[]{:S(2)}) collective-permute-start(s16[528,512]{1,0:T(8,128)(2,1)} %get-tuple-element.64), channel_id=1, source_target_pairs={{0,1},{1,0},{2,3},{3,2},{4,5},{5,4},{6,7},{7,6},{8,9},{9,8},{10,11... | collective-permute-start | bytes 1622024 | tf_op jit(solution)/shard_map/ppermute | solution.py:215
  138.4 12.0 %collective-permute-start.17 = (s16[208,512]{1,0:T(8,128)(2,1)S(1)}, s16[208,512]{1,0:T(8,128)(2,1)S(1)}, u32[]{:S(2)}, u32[]{:S(2)}) collective-permute-start(s16[208,512]{1,0:T(8,128)(2,1)S(1)} %copy-done.29), channel_id=1, source_target_pairs={{0,2},{1,3},{2,0},{3,1},{4,6},{5,7},{6,4},{7,5},{8,10},{9,11},{10,... | collective-permute-start | bytes 638984 | tf_op jit(solution)/shard_map/ppermute | solution.py:215
  139.9 17.7 %collective-permute-start.18 = (s16[208,512]{1,0:T(8,128)(2,1)S(1)}, s16[208,512]{1,0:T(8,128)(2,1)S(1)}, u32[]{:S(2)}, u32[]{:S(2)}) collective-permute-start(s16[208,512]{1,0:T(8,128)(2,1)S(1)} %copy-done.28), channel_id=1, source_target_pairs={{0,4},{1,5},{2,6},{3,7},{4,0},{5,1},{6,2},{7,3},{8,12},{9,13},{10,... | collective-permute-start | bytes 638984 | tf_op jit(solution)/shard_map/ppermute | solution.py:215
  141.9 16.8 %collective-permute-start.19 = (s16[208,512]{1,0:T(8,128)(2,1)S(1)}, s16[208,512]{1,0:T(8,128)(2,1)S(1)}, u32[]{:S(2)}, u32[]{:S(2)}) collective-permute-start(s16[208,512]{1,0:T(8,128)(2,1)S(1)} %copy-done.27), channel_id=1, source_target_pairs={{0,6},{1,7},{2,4},{3,5},{4,2},{5,3},{6,0},{7,1},{8,14},{9,15},{10,... | collective-permute-start | bytes 638984 | tf_op jit(solution)/shard_map/ppermute | solution.py:215
  147.1 27.1 %collective-permute-start.24 = (s16[208,512]{1,0:T(8,128)(2,1)}, s16[208,512]{1,0:T(8,128)(2,1)S(1)}, u32[]{:S(2)}, u32[]{:S(2)}) collective-permute-start(s16[208,512]{1,0:T(8,128)(2,1)} %get-tuple-element.61), channel_id=1, source_target_pairs={{0,2},{1,3},{2,0},{3,1},{4,6},{5,7},{6,4},{7,5},{8,10},{9,11},{10,... | collective-permute-start | bytes 638984 | tf_op jit(solution)/shard_map/ppermute | solution.py:215
  150.4 39.9 %copy-start.15 = (s16[208,512]{1,0:T(8,128)(2,1)}, s16[208,512]{1,0:T(8,128)(2,1)S(1)}, u32[]{:S(2)}) copy-start(s16[208,512]{1,0:T(8,128)(2,1)S(1)} %collective-permute-done.17.refs_1_) | copy-start | bytes 638980
  150.4 32.2 %collective-permute-start.25 = (s16[208,512]{1,0:T(8,128)(2,1)}, s16[208,512]{1,0:T(8,128)(2,1)S(1)}, u32[]{:S(2)}, u32[]{:S(2)}) collective-permute-start(s16[208,512]{1,0:T(8,128)(2,1)} %get-tuple-element.62), channel_id=1, source_target_pairs={{0,4},{1,5},{2,6},{3,7},{4,0},{5,1},{6,2},{7,3},{8,12},{9,13},{10,... | collective-permute-start | bytes 638984 | tf_op jit(solution)/shard_map/ppermute | solution.py:215
  151.7 30.9 %collective-permute-start.26 = (s16[208,512]{1,0:T(8,128)(2,1)}, s16[208,512]{1,0:T(8,128)(2,1)S(1)}, u32[]{:S(2)}, u32[]{:S(2)}) collective-permute-start(s16[208,512]{1,0:T(8,128)(2,1)} %get-tuple-element.63), channel_id=1, source_target_pairs={{0,6},{1,7},{2,4},{3,5},{4,2},{5,3},{6,0},{7,1},{8,14},{9,15},{10,... | collective-permute-start | bytes 638984 | tf_op jit(solution)/shard_map/ppermute | solution.py:215
  157.5 32.8 %copy-start.16 = (s16[208,512]{1,0:T(8,128)(2,1)}, s16[208,512]{1,0:T(8,128)(2,1)S(1)}, u32[]{:S(2)}) copy-start(s16[208,512]{1,0:T(8,128)(2,1)S(1)} %collective-permute-done.18.refs_2_) | copy-start | bytes 638980
  157.5 25.1 %collective-permute-start.28 = (s16[144,512]{1,0:T(8,128)(2,1)}, s16[144,512]{1,0:T(8,128)(2,1)S(1)}, u32[]{:S(2)}, u32[]{:S(2)}) collective-permute-start(s16[144,512]{1,0:T(8,128)(2,1)} %get-tuple-element.66), channel_id=1, source_target_pairs={{0,2},{1,3},{2,0},{3,1},{4,6},{5,7},{6,4},{7,5},{8,10},{9,11},{10,... | collective-permute-start | bytes 442376 | tf_op jit(solution)/shard_map/ppermute | solution.py:215
  158.6 31.7 %copy-start.17 = (s16[208,512]{1,0:T(8,128)(2,1)}, s16[208,512]{1,0:T(8,128)(2,1)S(1)}, u32[]{:S(2)}) copy-start(s16[208,512]{1,0:T(8,128)(2,1)S(1)} %collective-permute-done.19.refs_3_) | copy-start | bytes 638980
  158.6 31.7 %collective-permute-start.29 = (s16[144,512]{1,0:T(8,128)(2,1)}, s16[144,512]{1,0:T(8,128)(2,1)S(1)}, u32[]{:S(2)}, u32[]{:S(2)}) collective-permute-start(s16[144,512]{1,0:T(8,128)(2,1)} %get-tuple-element.67), channel_id=1, source_target_pairs={{0,4},{1,5},{2,6},{3,7},{4,0},{5,1},{6,2},{7,3},{8,12},{9,13},{10,... | collective-permute-start | bytes 442376 | tf_op jit(solution)/shard_map/ppermute | solution.py:215
  174.2 16.1 %copy-start.18 = (s16[208,512]{1,0:T(8,128)(2,1)}, s16[208,512]{1,0:T(8,128)(2,1)S(1)}, u32[]{:S(2)}) copy-start(s16[208,512]{1,0:T(8,128)(2,1)S(1)} %collective-permute-done.24.refs_5_) | copy-start | bytes 638980
  174.2 16.1 %collective-permute-start.30 = (s16[144,512]{1,0:T(8,128)(2,1)}, s16[144,512]{1,0:T(8,128)(2,1)S(1)}, u32[]{:S(2)}, u32[]{:S(2)}) collective-permute-start(s16[144,512]{1,0:T(8,128)(2,1)} %get-tuple-element.68), channel_id=1, source_target_pairs={{0,6},{1,7},{2,4},{3,5},{4,2},{5,3},{6,0},{7,1},{8,14},{9,15},{10,... | collective-permute-start | bytes 442376 | tf_op jit(solution)/shard_map/ppermute | solution.py:215
  182.6 7.8 %copy-start.20 = (s16[208,512]{1,0:T(8,128)(2,1)}, s16[208,512]{1,0:T(8,128)(2,1)S(1)}, u32[]{:S(2)}) copy-start(s16[208,512]{1,0:T(8,128)(2,1)S(1)} %collective-permute-done.26.refs_7_) | copy-start | bytes 638980
  182.6 7.8 %copy-start.21 = (s16[144,512]{1,0:T(8,128)(2,1)}, s16[144,512]{1,0:T(8,128)(2,1)S(1)}, u32[]{:S(2)}) copy-start(s16[144,512]{1,0:T(8,128)(2,1)S(1)} %collective-permute-done.28.refs_9_) | copy-start | bytes 442372
  (13 other events, 28.0 us)
